TPU v7x, 32 devices: a whole 2x2x4 slice. The times are simulated.
32 devices in a mesh: section: 4 (over z), rep: 8 (over y, x, core).
Axes of the slice: x: 2, y: 2, z: 4, core: 2. Of those that a mesh axis runs over, the one named last changes fastest.
Arguments:
- cache: bfloat16 [4, 4096, 3584], P('section', 'rep'), may hold values from -6 to 6
- payload: bfloat16 [4, 4096, 3584], P('section', 'rep'), may hold values from -6 to 6
- block_ids: int32 [4, 8, 2], P('section', 'rep'), may hold values from 0 to 3, as said below
- block_counts: int32 [4, 8], P('section', 'rep'), may hold values from 1 to 2, as said below
- block_scales: int32 [4, 8, 2], P('section', 'rep'), may hold values from 1024 to 8192
- refresh_ids: int32 [4, 8, 128], P('section', 'rep'), may hold values from 0 to 511, as said below
- refresh_counts: int32 [4, 8], P('section', 'rep'), may hold values from 1 to 128, as said below
- norm_gain: float32 [4, 3584], P('section'), may hold values from 0.5 to 1.5
- query_weight: bfloat16 [4, 3584, 3584], P('section', 'rep'), may hold values from -0.09375 to 0.09375
- query_bias: float32 [4, 3584], P('section'), may hold values from -3 to 3
- kv_weight: bfloat16 [4, 3584, 1024], P('section', 'rep'), may hold values from -0.09375 to 0.09375
- kv_bias: float32 [4, 1024], P('section'), may hold values from -3 to 3
Outputs:
- rebuilt: bfloat16 [4, 4096, 3584], P('section', 'rep')
- queries: bfloat16 [4, 4096, 3584], P('section', 'rep')
- keys_values: bfloat16 [4, 4096, 1024], P('section', 'rep')
Inputs may be any that keep to these rules, and one draw needn't show every extreme that they name: `block_ids`: for each section and relay the 2 entries are different block numbers; only the first block_counts entries are used. `block_counts`: in every section some relay lists exactly 2 blocks. `refresh_ids`: for each section and relay the entries are different local row numbers; only the first refresh_counts entries are used. `refresh_counts`: in every section some relay lists exactly 128 rows.
All inputs are finite; a program needn't handle non-finite values.
Results may differ from a plain program's by a relative error of at most 0.0052.
Values may be sent and summed in bfloat16 or wider, within the bound.
A program may use at most 256 MiB of HBM per device.

v0:
```python
import jax
import jax.numpy as jnp
from jax import lax
from jax.sharding import PartitionSpec as P

BLK = 128


EPSILON = 1e-06


def passed_along(block, axis, distance):
    devices = range(lax.axis_size(axis))
    route = [(i - distance, i) for i in devices if i - distance in devices]
    return lax.ppermute(block, axis, route)


def live_factor(got_ids, got_counts, got_scales):
    live = jnp.arange(got_ids.shape[0]) < got_counts
    return jnp.where(live, got_scales.astype(jnp.float32) / 4096.0, 0.0)


def live_rows(got_rows, got_rcounts, row_count):
    live = jnp.arange(got_rows.shape[0]) < got_rcounts
    return (got_rows[:, None] == jnp.arange(row_count)[None, :]) & live[:, None]


def body(
    cache,
    payload,
    block_ids,
    block_counts,
    block_scales,
    refresh_ids,
    refresh_counts,
    norm_gain,
    query_weight,
    query_bias,
    kv_weight,
    kv_bias,
):
    row_count = cache.shape[1]
    feature = cache.shape[2]
    blocks = row_count // BLK
    stored = cache[0].astype(jnp.float32)
    arrived = passed_along(
        (payload, block_ids, block_counts, block_scales, refresh_ids, refresh_counts), "section", 1
    )
    values, got_ids, got_counts, got_scales, got_rows, got_rcounts = arrived
    factor = live_factor(got_ids[0, 0], got_counts[0, 0], got_scales[0, 0])
    select = (got_ids[0, 0][:, None] == jnp.arange(blocks)[None, :]).astype(jnp.float32)
    per_block = jnp.sum(factor[:, None] * select, axis=0)
    shaped = values[0].reshape(blocks, BLK, feature).astype(jnp.float32)
    delta = (shaped * per_block[:, None, None]).astype(jnp.bfloat16)
    delta = lax.optimization_barrier(delta).astype(jnp.float32).reshape(row_count, feature)
    matches = live_rows(got_rows[0, 0], got_rcounts[0, 0], row_count)
    hit = jnp.any(matches, axis=0)
    mixed = jnp.where(hit[:, None], values[0].astype(jnp.float32), stored + delta)
    rebuilt = mixed.astype(jnp.bfloat16)
    wide = rebuilt.astype(jnp.float32)
    scale_rows = lax.rsqrt(jnp.mean(wide * wide, axis=1, keepdims=True) + EPSILON)
    normed = (wide * scale_rows * norm_gain[0][None, :]).astype(jnp.bfloat16)

    def add_rows(piece):
        return jnp.dot(normed, piece[0], preferred_element_type=jnp.float32)

    query_sum = add_rows(lax.all_gather(query_weight, "rep", axis=1, tiled=True))
    kv_sum = add_rows(lax.all_gather(kv_weight, "rep", axis=1, tiled=True))
    queries = (query_sum + query_bias[0][None, :]).astype(jnp.bfloat16)
    keys_values = (kv_sum + kv_bias[0][None, :]).astype(jnp.bfloat16)
    return (rebuilt[None], queries[None], keys_values[None])


def solution(mesh):
    in_specs = (
        P("section", "rep", None),
        P("section", "rep", None),
        P("section", "rep", None),
        P("section", "rep"),
        P("section", "rep", None),
        P("section", "rep", None),
        P("section", "rep"),
        P("section", None),
        P("section", "rep", None),
        P("section", None),
        P("section", "rep", None),
        P("section", None),
    )
    out_specs = (P("section", "rep", None), P("section", "rep", None), P("section", "rep", None))
    return jax.shard_map(body, mesh=mesh, in_specs=in_specs, out_specs=out_specs, check_vma=False)
```

profile of v0, /device:TPU:0, one launch (start us, length us, event | category | flops | bytes accessed | tf_op | source)
XLA Modules:
  0.0 219.3 jit_solution(1258083469612909675)
XLA Ops:
  7.2 0.0 all-gather.5.cloned.1.call-start
  7.2 0.7 all-gather.5.cloned.1.call-update
  7.9 0.0 all-gather.3.cloned.1.call-start
  7.9 0.7 all-gather.3.cloned.1.call-update
  8.7 6.7 %collective-permute-start.2 = (bf16[1,512,3584]{2,1,0:T(8,128)(2,1)}, bf16[1,512,3584]{2,1,0:T(8,128)(2,1)}, u32[]{:S(2)}, u32[]{:S(2)}) collective-permute-start(bf16[1,512,3584]{2,1,0:T(8,128)(2,1)} %param.13), channel_id=1, source_target_pairs={{0,8},{8,16},{16,24},{1,9},{9,17},{17,25},{2,10},{10,18},{18,26},{... | collective-permute-start | bytes 11010056 | tf_op jit(solution)/shard_map/ppermute | solution.py:15
  15.4 2.2 %collective-permute-start.4 = (s32[1,1]{1,0:T(1,128)}, s32[1,1]{1,0:T(1,128)}, u32[]{:S(2)}, u32[]{:S(2)}) collective-permute-start(s32[1,1]{1,0:T(1,128)} %param.15), channel_id=1, source_target_pairs={{0,8},{8,16},{16,24},{1,9},{9,17},{17,25},{2,10},{10,18},{18,26},{... | collective-permute-start | bytes 20 | tf_op jit(solution)/shard_map/ppermute | solution.py:15
  17.6 3.0 %collective-permute-start.5 = (s32[1,1,2]{2,1,0:T(1,128)}, s32[1,1,2]{2,1,0:T(1,128)S(1)}, u32[]{:S(2)}, u32[]{:S(2)}) collective-permute-start(s32[1,1,2]{2,1,0:T(1,128)} %param.16), channel_id=1, source_target_pairs={{0,8},{8,16},{16,24},{1,9},{9,17},{17,25},{2,10},{10,18},{18,26},{... | collective-permute-start | bytes 32 | tf_op jit(solution)/shard_map/ppermute | solution.py:15
  20.6 1.9 collective-permute-start.3
  22.5 2.4 %collective-permute-start.1 = (s32[1,1]{1,0:T(1,128)}, s32[1,1]{1,0:T(1,128)}, u32[]{:S(2)}, u32[]{:S(2)}) collective-permute-start(s32[1,1]{1,0:T(1,128)} %param.18), channel_id=1, source_target_pairs={{0,8},{8,16},{16,24},{1,9},{9,17},{17,25},{2,10},{10,18},{18,26},{... | collective-permute-start | bytes 20 | tf_op jit(solution)/shard_map/ppermute | solution.py:15
  25.0 0.8 reduce
  25.7 0.8 reduce.1
  26.5 66.1 %collective-permute-done.1 = s32[1,1]{1,0:T(1,128)} collective-permute-done((s32[1,1]{1,0:T(1,128)}, s32[1,1]{1,0:T(1,128)}, u32[]{:S(2)}, u32[]{:S(2)}) %collective-permute-start.1) | collective-permute-done | bytes 36 | tf_op jit(solution)/shard_map/ppermute | solution.py:15
  92.5 4.5 %collective-permute-start = (s32[1,1,128]{2,1,0:T(1,128)}, s32[1,1,128]{2,1,0:T(1,128)S(1)}, u32[]{:S(2)}, u32[]{:S(2)}) collective-permute-start(s32[1,1,128]{2,1,0:T(1,128)} %param.17), channel_id=1, source_target_pairs={{0,8},{8,16},{16,24},{1,9},{9,17},{17,25},{2,10},{10,18},{18,26},{... | collective-permute-start | bytes 1544 | tf_op jit(solution)/shard_map/ppermute | solution.py:15
  97.0 0.6 iota_compare_fusion.1
  97.6 0.0 collective-permute-done.4
  97.6 0.0 collective-permute-done.5
  97.6 0.6 compare_select_fusion
  98.3 0.0 collective-permute-done.3
  98.3 0.1 fusion.24
  98.4 0.1 collective-permute-done
  98.4 0.1 fusion.23
  98.5 0.0 collective-permute-done.2
  98.6 2.8 %multiply_convert_fusion.1 = bf16[4,128,3584]{2,1,0:T(8,128)(2,1)S(1)} fusion(f32[4]{0:T(128)S(1)} %fusion.24, bf16[4,128,3584]{2,1,0:T(8,128)(2,1)} %bitcast.50), kind=kLoop, calls=%fused_computation.14 | loop fusion | flops 5505024 | bytes 7340048 | tf_op jit(solution)/shard_map/convert_element_type | solution.py:54
  101.4 0.0 copy-start
  101.4 0.9 convert_element_type.77
  102.3 1.1 copy-done
  103.4 3.6 %multiply_reduce_fusion = f32[512]{0:T(512)S(1)} fusion(bf16[1,512,3584]{2,1,0:T(8,128)(2,1)S(1)} %copy-done, bf16[1,512,3584]{2,1,0:T(8,128)(2,1)} %collective-permute-done.2, pred[512]{0:T(512)(128)(4,1)S(1)} %fusion.23, bf16[4,128,3584]{2,1,0:T(8,128)(2,1)S(1)} %multiply_convert_fusion.1), kind=kLoop, calls=%fused_computation.13 | loop fusion | flops 16514560 | bytes 11012608 | tf_op jit(solution)/shard_map/reduce_sum | solution.py:61
  107.0 0.0 copy-start.1
  107.0 5.7 %fusion.3 = bf16[1,512,3584]{2,1,0:T(8,128)(2,1)} fusion(bf16[1,512,3584]{2,1,0:T(8,128)(2,1)S(1)} %copy-done, bf16[1,512,3584]{2,1,0:T(8,128)(2,1)} %collective-permute-done.2, pred[512]{0:T(512)(128)(4,1)S(1)} %fusion.23, f32[1,512,3584]{2,1,0:T(8,128)S(1)} %bitcast.52), kind=kLoop, calls=%fused_computation.5 | loop fusion | flops 9175040 | bytes 18350592 | tf_op jit(solution)/shard_map/convert_element_type | solution.py:59
  112.7 9.2 %fusion.17 = bf16[1,512,1024]{2,1,0:T(8,128)(2,1)} fusion(bf16[1,3584,1024]{2,1,0:T(8,128)(2,1)} %all-gather.5.cloned.1.call-done, bf16[1,512,3584]{2,1,0:T(8,128)(2,1)} %fusion.3, f32[3584]{0:T(1024)S(1)} %reduce, f32[512]{0:T(512)S(1)} %add_rsqrt_fusion, f32[1024]{0:T(1024)S(1)} %bitcast.53), kind=kOutput, calls=%fused_computation.18 | convolution fusion | flops 3766484992 | bytes 12079104 | tf_op jit(solution)/shard_map/dot_general | solution.py:65
  121.9 69.9 %all-gather.3.cloned.1.call-done = bf16[1,3584,3584]{2,1,0:T(8,128)(2,1)} async-done(((bf16[1,448,3584]{2,1,0:T(8,128)(2,1)}), bf16[1,3584,3584]{2,1,0:T(8,128)(2,1)}) %all-gather.3.cloned.1.call-update) | async-done | bytes 25690128 | tf_op jit(solution)/shard_map/all_gather | solution.py:67
  191.8 20.7 %fusion.11 = bf16[1,512,3584]{2,1,0:T(8,128)(2,1)} fusion(bf16[1,3584,3584]{2,1,0:T(8,128)(2,1)} %all-gather.3.cloned.1.call-done, f32[3584]{0:T(1024)S(1)} %reduce.1, bf16[1,512,3584]{2,1,0:T(8,128)(2,1)} %fusion.3, f32[3584]{0:T(1024)S(1)} %reduce, f32[512]{0:T(512)S(1)} %add_rsqrt_fusion), kind=kOutput, calls=%fused_computation.15 | convolution fusion | flops 13164347392 | bytes 33060864 | tf_op jit(solution)/shard_map/dot_general | solution.py:65
  (3 shorter events, 0.0 us)
Async XLA Ops:
  7.2 105.6 %all-gather.5.cloned.1.call-start = ((), (), s32[]{:S(2)}) async-start(), calls=%async_computation.1 | async-start | bytes 8257536 | tf_op jit(solution)/shard_map/all_gather | solution.py:68
  7.9 183.9 %all-gather.3.cloned.1.call-start = ((), (), s32[]{:S(2)}) async-start(), calls=%async_computation | async-start | bytes 28901376 | tf_op jit(solution)/shard_map/all_gather | solution.py:67
  8.7 89.9 %collective-permute-start.2 = (bf16[1,512,3584]{2,1,0:T(8,128)(2,1)}, bf16[1,512,3584]{2,1,0:T(8,128)(2,1)}, u32[]{:S(2)}, u32[]{:S(2)}) collective-permute-start(bf16[1,512,3584]{2,1,0:T(8,128)(2,1)} %param.13), channel_id=1, source_target_pairs={{0,8},{8,16},{16,24},{1,9},{9,17},{17,25},{2,10},{10,18},{18,26},{... | collective-permute-start | bytes 11010056 | tf_op jit(solution)/shard_map/ppermute | solution.py:15
  15.4 82.2 %collective-permute-start.4 = (s32[1,1]{1,0:T(1,128)}, s32[1,1]{1,0:T(1,128)}, u32[]{:S(2)}, u32[]{:S(2)}) collective-permute-start(s32[1,1]{1,0:T(1,128)} %param.15), channel_id=1, source_target_pairs={{0,8},{8,16},{16,24},{1,9},{9,17},{17,25},{2,10},{10,18},{18,26},{... | collective-permute-start | bytes 20 | tf_op jit(solution)/shard_map/ppermute | solution.py:15
  17.6 80.0 %collective-permute-start.5 = (s32[1,1,2]{2,1,0:T(1,128)}, s32[1,1,2]{2,1,0:T(1,128)S(1)}, u32[]{:S(2)}, u32[]{:S(2)}) collective-permute-start(s32[1,1,2]{2,1,0:T(1,128)} %param.16), channel_id=1, source_target_pairs={{0,8},{8,16},{16,24},{1,9},{9,17},{17,25},{2,10},{10,18},{18,26},{... | collective-permute-start | bytes 32 | tf_op jit(solution)/shard_map/ppermute | solution.py:15
  20.6 77.7 %collective-permute-start.3 = (s32[1,1,2]{2,1,0:T(1,128)}, s32[1,1,2]{2,1,0:T(1,128)S(1)}, u32[]{:S(2)}, u32[]{:S(2)}) collective-permute-start(s32[1,1,2]{2,1,0:T(1,128)} %param.14), channel_id=1, source_target_pairs={{0,8},{8,16},{16,24},{1,9},{9,17},{17,25},{2,10},{10,18},{18,26},{... | collective-permute-start | bytes 32 | tf_op jit(solution)/shard_map/ppermute | solution.py:15
  22.5 70.0 %collective-permute-start.1 = (s32[1,1]{1,0:T(1,128)}, s32[1,1]{1,0:T(1,128)}, u32[]{:S(2)}, u32[]{:S(2)}) collective-permute-start(s32[1,1]{1,0:T(1,128)} %param.18), channel_id=1, source_target_pairs={{0,8},{8,16},{16,24},{1,9},{9,17},{17,25},{2,10},{10,18},{18,26},{... | collective-permute-start | bytes 20 | tf_op jit(solution)/shard_map/ppermute | solution.py:15
  92.5 5.9 %collective-permute-start = (s32[1,1,128]{2,1,0:T(1,128)}, s32[1,1,128]{2,1,0:T(1,128)S(1)}, u32[]{:S(2)}, u32[]{:S(2)}) collective-permute-start(s32[1,1,128]{2,1,0:T(1,128)} %param.17), channel_id=1, source_target_pairs={{0,8},{8,16},{16,24},{1,9},{9,17},{17,25},{2,10},{10,18},{18,26},{... | collective-permute-start | bytes 1544 | tf_op jit(solution)/shard_map/ppermute | solution.py:15
  101.4 2.0 copy-start
  107.0 5.7 %copy-start.1 = (f32[1,1024]{1,0:T(1,128)S(1)}, f32[1,1024]{1,0:T(1,128)}, u32[]{:S(2)}) copy-start(f32[1,1024]{1,0:T(1,128)} %param.23) | copy-start | bytes 12292
Sparse Core Ops, SparseCore 0:
  9.9 52.5 all-gather.4
  64.3 127.3 all-gather.2
where the time goes:
time: 220 us; the launch traced here: 219 us
  waiting for transfers between devices  137 us (62%)
  matrix products  29.9 us (14%)
  starting transfers between devices  20.9 us (10%)
  other arithmetic  16 us (7%)
  between operations  14.2 us (6%)
    all_gather x1, waiting for transfers between devices, body(): lax.all_gather(query_weight, 'rep', axis=1, tiled=True)  69.9 us
    ppermute x6, waiting for transfers between devices, passed_along(): return lax.ppermute(block, axis, route)  66.1 us
    dot_general x2, matrix products, add_rows(): return jnp.dot(normed, piece[0], preferred_element_type=jnp.float32)  29.9 us
    ppermute x6, starting transfers between devices, passed_along(): return lax.ppermute(block, axis, route)  20.8 us
    convert_element_type x1, other arithmetic, body(): rebuilt = mixed.astype(jnp.bfloat16)  5.7 us
  transfers between devices with their start and end apart: 8, of which 3 were waited for; matrix products, arithmetic and copies ran while one was open for 11% of the time, Pallas kernels for 0%

commit v1 on v0

v1 whole, which is shorter than its diff:
```python
import functools

import jax
import jax.numpy as jnp
from jax import lax
from jax.experimental import pallas as pl
from jax.experimental.pallas import tpu as pltpu
from jax.sharding import PartitionSpec as P

BLK = 128
CW = 256
TILE = 16
EPSILON = 1e-06
MESH = pl.DeviceIdType.MESH


def chip_at(pos, chips):
    half = chips // 2
    back = pos // half
    return pos + back * (half + chips - 1 - 2 * pos)


def kernel(
    sections,
    reps,
    most_blk,
    meta_ref,
    payload_ref,
    cache_ref,
    gain_ref,
    qw_ref,
    qb_ref,
    kvw_ref,
    kvb_ref,
    rebuilt_ref,
    q_ref,
    kv_ref,
    w,
    values,
    stored,
    normed,
    staged,
    bias,
    meta,
    local_sem,
    keep_sem,
    row_send,
    row_recv,
    own_send,
    pair_own_recv,
    ring_send,
    ring_recv,
    pair_send,
    pair_recv,
    out_sem,
):
    chips = reps // 2
    hops = chips // 2
    depth = qw_ref.shape[1]
    rows = payload_ref.shape[1]
    feature = payload_ref.shape[2]
    nq = qw_ref.shape[2] // CW
    nc = nq + kvw_ref.shape[2] // CW
    nh = nc // 2
    row_chunks = rows // BLK

    section = lax.axis_index("section")
    me = lax.axis_index("rep")
    core = me % 2
    chip = me // 2
    pos = chip + (chip // hops) * (hops + chips - 1 - 2 * chip)
    partner = 2 * chip + (1 - core)

    def rep_at(place, which):
        return 2 * chip_at((place + chips) % chips, chips) + which

    towards = (rep_at(pos + 1, core), rep_at(pos - 1, core))

    barrier = pltpu.get_barrier_semaphore()
    for other in (partner,) + towards:
        pl.semaphore_signal(barrier, 1, device_id={"rep": other}, device_id_type=MESH)

    @pl.when(section > 0)
    def _():
        pl.semaphore_signal(
            barrier, 1, device_id={"section": section - 1}, device_id_type=MESH
        )

    @pl.when(section < sections - 1)
    def _():
        pl.semaphore_signal(
            barrier, 1, device_id={"section": section + 1}, device_id_type=MESH
        )

    def own(c):
        if c < nq:
            return qw_ref.at[0, :, pl.ds(c * CW, CW)]
        return kvw_ref.at[0, :, pl.ds((c - nq) * CW, CW)]

    def slot(c, block):
        return w.at[c, pl.ds(pl.multiple_of(block * depth, depth), depth), :]

    keep = pltpu.make_async_copy(cache_ref.at[0], stored, keep_sem)
    keep.start()
    own_locals = [
        pltpu.make_async_copy(own(c), slot(c, me), local_sem.at[c]) for c in range(nc)
    ]

    sides = (section + sections - 1) // sections + (2 * sections - 2 - section) // sections
    pl.semaphore_wait(barrier, 3 + sides)

    def meta_copy():
        return pltpu.make_async_remote_copy(
            src_ref=meta_ref,
            dst_ref=meta,
            send_sem=row_send.at[row_chunks],
            recv_sem=row_recv.at[row_chunks],
            device_id={"section": section + 1},
            device_id_type=MESH,
        )

    def row_copy(j):
        return pltpu.make_async_remote_copy(
            src_ref=payload_ref.at[0, pl.ds(j * BLK, BLK), :],
            dst_ref=values.at[pl.ds(j * BLK, BLK), :],
            send_sem=row_send.at[j],
            recv_sem=row_recv.at[j],
            device_id={"section": section + 1},
            device_id_type=MESH,
        )

    @pl.when(section < sections - 1)
    def _():
        meta_copy().start()
        for j in range(row_chunks):
            row_copy(j).start()

    for c in range(nc):
        for d in range(2):
            pltpu.make_async_remote_copy(
                src_ref=own(c),
                dst_ref=slot(c, me),
                send_sem=own_send.at[d],
                recv_sem=ring_recv.at[d, 0, c],
                device_id={"rep": towards[d]},
                device_id_type=MESH,
            ).start()
        pltpu.make_async_remote_copy(
            src_ref=own(c),
            dst_ref=slot(c, me),
            send_sem=own_send.at[2],
            recv_sem=pair_own_recv.at[c],
            device_id={"rep": partner},
            device_id_type=MESH,
        ).start()
        own_locals[c].start()

    @pl.when(section == 0)
    def _():
        meta[...] = jnp.zeros_like(meta)

        @pl.loop(0, rows // TILE)
        def _(i):
            values[pl.ds(i * TILE, TILE), :] = jnp.zeros((TILE, feature), values.dtype)

    for c in range(nq):
        bias[c] = qb_ref[:, c * CW : (c + 1) * CW]
    for c in range(nq, nc):
        bias[c] = kvb_ref[:, (c - nq) * CW : (c - nq + 1) * CW]
    keep.wait()
    for c in range(nc):
        own_locals[c].wait()

    def block_of(d, t, which):
        return rep_at(pos - t if d == 0 else pos + t, which)

    def landed(sem, c, block):
        pltpu.make_async_copy(slot(c, block), slot(c, block), sem).wait()

    def to_pair(d, t, c):
        here = slot(c, block_of(d, t, core))
        pltpu.make_async_remote_copy(
            src_ref=here,
            dst_ref=here,
            send_sem=pair_send.at[d, t - 1],
            recv_sem=pair_recv.at[d, t - 1, c],
            device_id={"rep": partner},
            device_id_type=MESH,
        ).start()

    def onward(d, t, c):
        here = slot(c, block_of(d, t, core))
        pltpu.make_async_remote_copy(
            src_ref=here,
            dst_ref=here,
            send_sem=ring_send.at[d, t - 1],
            recv_sem=ring_recv.at[d, t, c],
            device_id={"rep": towards[d]},
            device_id_type=MESH,
        ).start()

    def rebuild(j):
        @pl.when(section > 0)
        def _():
            if j == 0:
                meta_copy().wait_recv()
            row_copy(j).wait_recv()

        count = meta[3:4, 0:1]
        factor = jnp.zeros((1, 1), jnp.float32)
        for i in range(most_blk):
            live = jnp.logical_and(meta[1:2, i : i + 1] == j, count > i)
            scale = meta[2:3, i : i + 1].astype(jnp.float32) / 4096.0
            factor = factor + jnp.where(live, scale, 0.0)

        @pl.loop(0, BLK // TILE)
        def _(i):
            first = j * BLK + i * TILE
            here = pl.ds(pl.multiple_of(first, TILE), TILE)
            ids = meta[0:1, :]
            lanes = lax.broadcasted_iota(jnp.int32, ids.shape, 1)
            ids = jnp.where(lanes < meta[4:5, :], ids, -1)
            number = first + lax.broadcasted_iota(jnp.int32, (TILE, ids.shape[1]), 0)
            match = jnp.where(ids == number, 1.0, 0.0)
            hit = jnp.max(match, axis=1, keepdims=True) > 0.0
            got = values[here, :].astype(jnp.float32)
            delta = (got * factor).astype(jnp.bfloat16).astype(jnp.float32)
            mixed = jnp.where(hit, got, stored[here, :].astype(jnp.float32) + delta)
            rebuilt = mixed.astype(jnp.bfloat16)
            stored[here, :] = rebuilt
            wide = rebuilt.astype(jnp.float32)
            mean = jnp.sum(wide * wide, axis=1, keepdims=True) / feature
            scale_rows = lax.rsqrt(mean + EPSILON)
            normed[here, :] = (wide * scale_rows * gain_ref[...]).astype(jnp.bfloat16)

    def rebuilt_out(j):
        here = pl.ds(j * BLK, BLK)
        return pltpu.make_async_copy(stored.at[here, :], rebuilt_ref.at[0, here, :], out_sem.at[j])

    marks = [(j + 1) * nc // row_chunks for j in range(row_chunks)]
    marks[-1] = nc
    for t in range(1, hops):
        done = 0
        for j, mark in enumerate(marks):

            @pl.loop(done, mark)
            def _(c):
                for d in range(2):
                    landed(ring_recv.at[d, t - 1, c], c, block_of(d, t, core))
                    if t + 1 < hops:
                        onward(d, t, c)
                    else:

                        @pl.when((c < nh) if d == 0 else (c >= nc - nh))
                        def _():
                            onward(d, t, c)

                    to_pair(d, t, c)

            done = mark
            if t == 1:
                rebuild(j)
                if j > 0:
                    rebuilt_out(j - 1).start()
    rebuilt_out(row_chunks - 1).start()

    def product(c, d):
        landed(pair_own_recv.at[c], c, partner)
        for t in range(1, hops):
            for e in range(2):
                landed(pair_recv.at[e, t - 1, c], c, block_of(e, t, 1 - core))
        landed(pair_recv.at[d, hops - 1, c], c, block_of(d, hops, 1 - core))
        total = jnp.dot(normed[...], w[c], preferred_element_type=jnp.float32)
        staged[c] = (total + bias[c]).astype(jnp.bfloat16)

    def result_out(c, start):
        def go(copy):
            copy.start() if start else copy.wait()

        @pl.when(c < nq)
        def _():
            go(
                pltpu.make_async_copy(
                    staged.at[c],
                    q_ref.at[0, :, pl.ds(pl.multiple_of(c * CW, CW), CW)],
                    out_sem.at[row_chunks + c],
                )
            )

        @pl.when(c >= nq)
        def _():
            go(
                pltpu.make_async_copy(
                    staged.at[c],
                    kv_ref.at[0, :, pl.ds(pl.multiple_of((c - nq) * CW, CW), CW)],
                    out_sem.at[row_chunks + c],
                )
            )

    @pl.loop(0, nh + 1)
    def _(i):
        @pl.when(i < nh)
        def _():
            for d in range(2):
                c = i + d * nh
                landed(ring_recv.at[d, hops - 1, c], c, block_of(d, hops, core))
                to_pair(d, hops, c)

        @pl.when(i > 0)
        def _():
            for d in range(2):
                c = i - 1 + d * nh
                product(c, d)
                result_out(c, True)

    @pl.loop(0, nc)
    def _(c):
        result_out(c, False)

    for j in range(row_chunks):
        rebuilt_out(j).wait()

    def sent(sem, count):
        part = w.at[pl.ds(0, count), pl.ds(0, depth), :]
        pltpu.make_async_copy(part, part, sem).wait()

    for k in range(3):
        sent(own_send.at[k], nc)
    for d in range(2):
        for t in range(1, hops):
            sent(ring_send.at[d, t - 1], nc if t + 1 < hops else nh)
            sent(pair_send.at[d, t - 1], nc)
        sent(pair_send.at[d, hops - 1], nh)

    @pl.when(section < sections - 1)
    def _():
        meta_copy().wait_send()
        for j in range(row_chunks):
            row_copy(j).wait_send()


def body(
    cache,
    payload,
    block_ids,
    block_counts,
    block_scales,
    refresh_ids,
    refresh_counts,
    norm_gain,
    query_weight,
    query_bias,
    kv_weight,
    kv_bias,
):
    sections = lax.axis_size("section")
    reps = lax.axis_size("rep")
    rows, feature = cache.shape[1:]
    depth = query_weight.shape[1]
    queries = query_weight.shape[2]
    keys = kv_weight.shape[2]
    most_blk = block_ids.shape[2]
    width = refresh_ids.shape[2]
    nc = (queries + keys) // CW
    hops = reps // 4
    row_chunks = rows // BLK

    def line(values):
        return jnp.pad(values[0], ((0, 0), (0, width - values.shape[2])))

    meta = jnp.concatenate(
        [
            refresh_ids[0],
            line(block_ids),
            line(block_scales),
            jnp.broadcast_to(block_counts, (1, width)),
            jnp.broadcast_to(refresh_counts, (4, width)),
        ],
        axis=0,
    )
    vmem = pl.BlockSpec(memory_space=pltpu.VMEM)
    anywhere = pl.BlockSpec(memory_space=pl.ANY)
    dma = pltpu.SemaphoreType.DMA
    return pl.pallas_call(
        functools.partial(kernel, sections, reps, most_blk),
        out_shape=(
            jax.ShapeDtypeStruct(cache.shape, cache.dtype),
            jax.ShapeDtypeStruct((1, rows, queries), cache.dtype),
            jax.ShapeDtypeStruct((1, rows, keys), cache.dtype),
        ),
        in_specs=[vmem, anywhere, anywhere, vmem, anywhere, vmem, anywhere, vmem],
        out_specs=(anywhere, anywhere, anywhere),
        scratch_shapes=[
            pltpu.VMEM((nc, reps * depth, CW), jnp.bfloat16),
            pltpu.VMEM((rows, feature), jnp.bfloat16),
            pltpu.VMEM((rows, feature), jnp.bfloat16),
            pltpu.VMEM((rows, feature), jnp.bfloat16),
            pltpu.VMEM((nc, rows, CW), jnp.bfloat16),
            pltpu.VMEM((nc, 1, CW), jnp.float32),
            pltpu.VMEM((8, width), jnp.int32),
            dma((nc,)),
            dma,
            dma((row_chunks + 1,)),
            dma((row_chunks + 1,)),
            dma((3,)),
            dma((nc,)),
            dma((2, hops)),
            dma((2, hops, nc)),
            dma((2, hops)),
            dma((2, hops, nc)),
            dma((row_chunks + nc,)),
        ],
        compiler_params=pltpu.CompilerParams(
            collective_id=0, has_side_effects=True, vmem_limit_bytes=60 * 1024 * 1024
        ),
    )(meta, payload, cache, norm_gain, query_weight, query_bias, kv_weight, kv_bias)


def solution(mesh):
    in_specs = (
        P("section", "rep", None),
        P("section", "rep", None),
        P("section", "rep", None),
        P("section", "rep"),
        P("section", "rep", None),
        P("section", "rep", None),
        P("section", "rep"),
        P("section", None),
        P("section", "rep", None),
        P("section", None),
        P("section", "rep", None),
        P("section", None),
    )
    out_specs = (P("section", "rep", None), P("section", "rep", None), P("section", "rep", None))
    return jax.shard_map(body, mesh=mesh, in_specs=in_specs, out_specs=out_specs, check_vma=False)
```

time: 220 us -> 162 us (0.74)
  Pallas kernels: 0 us -> 150 us
  waiting for transfers between devices: 137 us -> 0 us
  matrix products: 29.9 us -> 0 us
  starting transfers between devices: 20.9 us -> 0 us
  other arithmetic: 16 us -> 0 us
  between operations: 14.2 us -> 1.95 us
  local copies, waits for them, and re-layouts: 1.09 us -> 9.78 us
    pallas_call x0 -> x1, Pallas kernels: none -> 150 us  [body(): pl.pallas_call(functools.partial(kernel, sections, reps, most_blk), out_s...]
    all_gather x2 -> x0, waiting for transfers between devices: 69.9 us -> none  [the longest x1 69.9 us: body(): lax.all_gather(query_weight, 'rep', axis=1, tiled=True)]
    ppermute x6 -> x0, waiting for transfers between devices: 66.1 us -> none  [passed_along(): return lax.ppermute(block, axis, route)]
    dot_general x2 -> x0, matrix products: 29.9 us -> none  [add_rows(): return jnp.dot(normed, piece[0], preferred_element_type=jnp.float32)]
    ppermute x6 -> x0, starting transfers between devices: 20.8 us -> none  [passed_along(): return lax.ppermute(block, axis, route)]
    convert_element_type x3 -> x0, other arithmetic: 9.47 us -> none  [the longest x1 5.7 us: body(): rebuilt = mixed.astype(jnp.bfloat16)]
    unnamed x4 -> x7, local copies, waits for them, and re-layouts: 1.09 us -> 7.19 us
    reduce_sum x2 -> x0, other arithmetic: 3.65 us -> none  [the longest x1 3.57 us: body(): jnp.mean(wide * wide, axis=1, keepdims=True) + EPSILON]
  transfers between devices with their start and end apart: 8 -> 0, of which waited for: 3 -> 0; matrix products, arithmetic and copies ran while one was open for 11% -> 0% of each run, Pallas kernels for 0% -> 0%
where the time goes in v1:
time: 162 us
  Pallas kernels  150 us (93%)
  local copies, waits for them, and re-layouts  9.78 us (6%)
  between operations  1.95 us (1%)
    pallas_call x1, Pallas kernels, body(): pl.pallas_call(functools.partial(kernel, sections, reps, most_blk), out_s...  150 us
    unnamed x7, local copies, waits for them, and re-layouts  7.19 us

profile of v1, /device:TPU:0, one launch (start us, length us, event | category | flops | bytes accessed | tf_op | source)
XLA Modules:
  0.0 161.7 jit_solution(17200217546163151362)
XLA Ops:
  1.9 0.7 pad.7
  2.6 0.7 pad.8
  3.3 1.3 concatenate.3.meta_ref
  4.5 150.0 %shard_map.139 = (bf16[1,512,3584]{2,1,0:T(8,128)(2,1)}, bf16[1,512,3584]{2,1,0:T(8,128)(2,1)}, bf16[1,512,1024]{2,1,0:T(8,128)(2,1)}) custom-call(s32[8,128]{1,0:T(8,128)} %concatenate.3.meta_ref, bf16[1,512,3584]{2,1,0:T(8,128)(2,1)} %payload_ref.1, bf16[1,512,3584]{2,1,0:T(8,128)(2,1)} %cache_ref.1, f32[1,3584]{1,0:T(1,128)} %gain_ref.1, ...), custom_call_target="tpu_custom_call" | custom-call | tf_op jit(solution)/shard_map/pallas_call | solution.py:384
  154.5 0.0 copy-start
  154.6 4.3 %copy.20 = bf16[1,512,3584]{2,1,0:T(8,128)(2,1)} copy(bf16[1,512,3584]{2,1,0:T(8,128)(2,1)} %get-tuple-element.6) | data formatting | bytes 7340032
  158.8 0.0 copy-done
  158.8 0.0 copy-start.1
  158.8 1.8 %copy.21 = bf16[1,512,3584]{2,1,0:T(8,128)(2,1)} copy(bf16[1,512,3584]{2,1,0:T(8,128)(2,1)S(1)} %copy-done) | data formatting | bytes 7340032
  160.7 0.1 copy-done.1
  160.8 1.0 copy.22
  (2 shorter events, 0.0 us)
Async XLA Ops:
  154.5 4.3 %copy-start = (bf16[1,512,3584]{2,1,0:T(8,128)(2,1)S(1)}, bf16[1,512,3584]{2,1,0:T(8,128)(2,1)}, u32[]{:S(2)}) copy-start(bf16[1,512,3584]{2,1,0:T(8,128)(2,1)} %get-tuple-element.7) | copy-start | bytes 11010052
  158.8 2.0 %copy-start.1 = (bf16[1,512,1024]{2,1,0:T(8,128)(2,1)S(1)}, bf16[1,512,1024]{2,1,0:T(8,128)(2,1)}, u32[]{:S(2)}) copy-start(bf16[1,512,1024]{2,1,0:T(8,128)(2,1)} %get-tuple-element.8) | copy-start | bytes 3145732

commit v2 on v1

--- a/solution.py
+++ b/solution.py
@@ -24,7 +24,7 @@
     sections,
     reps,
     most_blk,
-    meta_ref,
+    lists_ref,
     payload_ref,
     cache_ref,
     gain_ref,
@@ -37,11 +37,10 @@
     kv_ref,
     w,
     values,
-    stored,
     normed,
-    staged,
+    sums,
     bias,
-    meta,
+    lists,
     local_sem,
     keep_sem,
     row_send,
@@ -52,7 +51,6 @@
     ring_recv,
     pair_send,
     pair_recv,
-    out_sem,
 ):
     chips = reps // 2
     hops = chips // 2
@@ -100,7 +98,7 @@
     def slot(c, block):
         return w.at[c, pl.ds(pl.multiple_of(block * depth, depth), depth), :]
 
-    keep = pltpu.make_async_copy(cache_ref.at[0], stored, keep_sem)
+    keep = pltpu.make_async_copy(cache_ref, rebuilt_ref, keep_sem)
     keep.start()
     own_locals = [
         pltpu.make_async_copy(own(c), slot(c, me), local_sem.at[c]) for c in range(nc)
@@ -109,12 +107,12 @@
     sides = (section + sections - 1) // sections + (2 * sections - 2 - section) // sections
     pl.semaphore_wait(barrier, 3 + sides)
 
-    def meta_copy():
+    def list_copy(i):
         return pltpu.make_async_remote_copy(
-            src_ref=meta_ref,
-            dst_ref=meta,
-            send_sem=row_send.at[row_chunks],
-            recv_sem=row_recv.at[row_chunks],
+            src_ref=lists_ref[i],
+            dst_ref=lists[i],
+            send_sem=row_send.at[row_chunks + i],
+            recv_sem=row_recv.at[row_chunks + i],
             device_id={"section": section + 1},
             device_id_type=MESH,
         )
@@ -131,7 +129,8 @@
 
     @pl.when(section < sections - 1)
     def _():
-        meta_copy().start()
+        for i in range(len(lists)):
+            list_copy(i).start()
         for j in range(row_chunks):
             row_copy(j).start()
 
@@ -157,7 +156,8 @@
 
     @pl.when(section == 0)
     def _():
-        meta[...] = jnp.zeros_like(meta)
+        for ref in lists:
+            ref[...] = jnp.zeros_like(ref)
 
         @pl.loop(0, rows // TILE)
         def _(i):
@@ -203,39 +203,39 @@
         @pl.when(section > 0)
         def _():
             if j == 0:
-                meta_copy().wait_recv()
+                for i in range(len(lists)):
+                    list_copy(i).wait_recv()
             row_copy(j).wait_recv()
 
-        count = meta[3:4, 0:1]
+        got_rows, got_ids, got_scales, got_counts, got_rcounts = lists
+        count = got_counts[...]
         factor = jnp.zeros((1, 1), jnp.float32)
         for i in range(most_blk):
-            live = jnp.logical_and(meta[1:2, i : i + 1] == j, count > i)
-            scale = meta[2:3, i : i + 1].astype(jnp.float32) / 4096.0
+            live = jnp.logical_and(got_ids[:, i : i + 1] == j, count > i)
+            scale = got_scales[:, i : i + 1].astype(jnp.float32) / 4096.0
             factor = factor + jnp.where(live, scale, 0.0)
 
         @pl.loop(0, BLK // TILE)
         def _(i):
             first = j * BLK + i * TILE
             here = pl.ds(pl.multiple_of(first, TILE), TILE)
-            ids = meta[0:1, :]
+            ids = got_rows[...]
             lanes = lax.broadcasted_iota(jnp.int32, ids.shape, 1)
-            ids = jnp.where(lanes < meta[4:5, :], ids, -1)
+            ids = jnp.where(lanes < got_rcounts[...], ids, -1)
             number = first + lax.broadcasted_iota(jnp.int32, (TILE, ids.shape[1]), 0)
             match = jnp.where(ids == number, 1.0, 0.0)
             hit = jnp.max(match, axis=1, keepdims=True) > 0.0
             got = values[here, :].astype(jnp.float32)
             delta = (got * factor).astype(jnp.bfloat16).astype(jnp.float32)
-            mixed = jnp.where(hit, got, stored[here, :].astype(jnp.float32) + delta)
+            mixed = jnp.where(hit, got, rebuilt_ref[0, here, :].astype(jnp.float32) + delta)
             rebuilt = mixed.astype(jnp.bfloat16)
-            stored[here, :] = rebuilt
+            rebuilt_ref[0, here, :] = rebuilt
             wide = rebuilt.astype(jnp.float32)
             mean = jnp.sum(wide * wide, axis=1, keepdims=True) / feature
             scale_rows = lax.rsqrt(mean + EPSILON)
-            normed[here, :] = (wide * scale_rows * gain_ref[...]).astype(jnp.bfloat16)
-
-    def rebuilt_out(j):
-        here = pl.ds(j * BLK, BLK)
-        return pltpu.make_async_copy(stored.at[here, :], rebuilt_ref.at[0, here, :], out_sem.at[j])
+            result = (wide * scale_rows * gain_ref[...]).astype(jnp.bfloat16)
+            for k in range(chips):
+                normed[k, here, :] = result[:, 2 * depth * k : 2 * depth * (k + 1)]
 
     marks = [(j + 1) * nc // row_chunks for j in range(row_chunks)]
     marks[-1] = nc
@@ -260,65 +260,54 @@
             done = mark
             if t == 1:
                 rebuild(j)
-                if j > 0:
-                    rebuilt_out(j - 1).start()
-    rebuilt_out(row_chunks - 1).start()
-
-    def product(c, d):
-        landed(pair_own_recv.at[c], c, partner)
-        for t in range(1, hops):
-            for e in range(2):
-                landed(pair_recv.at[e, t - 1, c], c, block_of(e, t, 1 - core))
-        landed(pair_recv.at[d, hops - 1, c], c, block_of(d, hops, 1 - core))
-        total = jnp.dot(normed[...], w[c], preferred_element_type=jnp.float32)
-        staged[c] = (total + bias[c]).astype(jnp.bfloat16)
-
-    def result_out(c, start):
-        def go(copy):
-            copy.start() if start else copy.wait()
-
-        @pl.when(c < nq)
+
+    far = chip_at((pos + hops) % chips, chips)
+    wide_depth = 2 * depth
+
+    def term(c, which):
+        rows_here = pl.ds(pl.multiple_of(which * wide_depth, wide_depth), wide_depth)
+        return jnp.dot(normed[which], w[c, rows_here, :], preferred_element_type=jnp.float32)
+
+    def partial(i):
+        for d in range(2):
+            c = i + d * nh
+            landed(pair_own_recv.at[c], c, partner)
+            for t in range(1, hops):
+                for e in range(2):
+                    landed(pair_recv.at[e, t - 1, c], c, block_of(e, t, 1 - core))
+            total = bias[c]
+            for step in range(1, chips):
+                total = total + term(c, (far + step) % chips)
+            sums[i % 2, d] = total
+
+    def finish(i):
+        for d in range(2):
+            c = i + d * nh
+            landed(pair_recv.at[d, hops - 1, c], c, block_of(d, hops, 1 - core))
+            result = (sums[i % 2, d] + term(c, far)).astype(jnp.bfloat16)
+
+            @pl.when(c < nq)
+            def _():
+                q_ref[0, :, pl.ds(pl.multiple_of(c * CW, CW), CW)] = result
+
+            @pl.when(c >= nq)
+            def _():
+                kv_ref[0, :, pl.ds(pl.multiple_of((c - nq) * CW, CW), CW)] = result
+
+    partial(0)
+
+    @pl.loop(0, nh)
+    def _(i):
+        for d in range(2):
+            c = i + d * nh
+            landed(ring_recv.at[d, hops - 1, c], c, block_of(d, hops, core))
+            to_pair(d, hops, c)
+
+        @pl.when(i + 1 < nh)
         def _():
-            go(
-                pltpu.make_async_copy(
-                    staged.at[c],
-                    q_ref.at[0, :, pl.ds(pl.multiple_of(c * CW, CW), CW)],
-                    out_sem.at[row_chunks + c],
-                )
-            )
-
-        @pl.when(c >= nq)
-        def _():
-            go(
-                pltpu.make_async_copy(
-                    staged.at[c],
-                    kv_ref.at[0, :, pl.ds(pl.multiple_of((c - nq) * CW, CW), CW)],
-                    out_sem.at[row_chunks + c],
-                )
-            )
-
-    @pl.loop(0, nh + 1)
-    def _(i):
-        @pl.when(i < nh)
-        def _():
-            for d in range(2):
-                c = i + d * nh
-                landed(ring_recv.at[d, hops - 1, c], c, block_of(d, hops, core))
-                to_pair(d, hops, c)
-
-        @pl.when(i > 0)
-        def _():
-            for d in range(2):
-                c = i - 1 + d * nh
-                product(c, d)
-                result_out(c, True)
-
-    @pl.loop(0, nc)
-    def _(c):
-        result_out(c, False)
-
-    for j in range(row_chunks):
-        rebuilt_out(j).wait()
+            partial(i + 1)
+
+        finish(i)
 
     def sent(sem, count):
         part = w.at[pl.ds(0, count), pl.ds(0, depth), :]
@@ -334,7 +323,8 @@
 
     @pl.when(section < sections - 1)
     def _():
-        meta_copy().wait_send()
+        for i in range(len(lists)):
+            list_copy(i).wait_send()
         for j in range(row_chunks):
             row_copy(j).wait_send()
 
@@ -360,60 +350,45 @@
     queries = query_weight.shape[2]
     keys = kv_weight.shape[2]
     most_blk = block_ids.shape[2]
-    width = refresh_ids.shape[2]
     nc = (queries + keys) // CW
     hops = reps // 4
     row_chunks = rows // BLK
 
-    def line(values):
-        return jnp.pad(values[0], ((0, 0), (0, width - values.shape[2])))
-
-    meta = jnp.concatenate(
-        [
-            refresh_ids[0],
-            line(block_ids),
-            line(block_scales),
-            jnp.broadcast_to(block_counts, (1, width)),
-            jnp.broadcast_to(refresh_counts, (4, width)),
-        ],
-        axis=0,
-    )
+    lists = (refresh_ids[0], block_ids[0], block_scales[0], block_counts, refresh_counts)
     vmem = pl.BlockSpec(memory_space=pltpu.VMEM)
-    anywhere = pl.BlockSpec(memory_space=pl.ANY)
+    anywhere = pl.BlockSpec(memory_space=pltpu.HBM)
     dma = pltpu.SemaphoreType.DMA
     return pl.pallas_call(
         functools.partial(kernel, sections, reps, most_blk),
         out_shape=(
-            jax.ShapeDtypeStruct(cache.shape, cache.dtype),
-            jax.ShapeDtypeStruct((1, rows, queries), cache.dtype),
-            jax.ShapeDtypeStruct((1, rows, keys), cache.dtype),
+            pltpu.VMEM(cache.shape, cache.dtype),
+            pltpu.VMEM((1, rows, queries), cache.dtype),
+            pltpu.VMEM((1, rows, keys), cache.dtype),
         ),
-        in_specs=[vmem, anywhere, anywhere, vmem, anywhere, vmem, anywhere, vmem],
-        out_specs=(anywhere, anywhere, anywhere),
+        in_specs=[(anywhere,) * len(lists), anywhere, anywhere, vmem, anywhere, vmem, anywhere, vmem],
+        out_specs=(vmem, vmem, vmem),
         scratch_shapes=[
             pltpu.VMEM((nc, reps * depth, CW), jnp.bfloat16),
             pltpu.VMEM((rows, feature), jnp.bfloat16),
-            pltpu.VMEM((rows, feature), jnp.bfloat16),
-            pltpu.VMEM((rows, feature), jnp.bfloat16),
-            pltpu.VMEM((nc, rows, CW), jnp.bfloat16),
+            pltpu.VMEM((reps // 2, rows, 2 * depth), jnp.bfloat16),
+            pltpu.VMEM((2, 2, rows, CW), jnp.float32),
             pltpu.VMEM((nc, 1, CW), jnp.float32),
-            pltpu.VMEM((8, width), jnp.int32),
+            tuple(pltpu.VMEM(x.shape, x.dtype) for x in lists),
             dma((nc,)),
             dma,
-            dma((row_chunks + 1,)),
-            dma((row_chunks + 1,)),
+            dma((row_chunks + len(lists),)),
+            dma((row_chunks + len(lists),)),
             dma((3,)),
             dma((nc,)),
             dma((2, hops)),
             dma((2, hops, nc)),
             dma((2, hops)),
             dma((2, hops, nc)),
-            dma((row_chunks + nc,)),
         ],
         compiler_params=pltpu.CompilerParams(
-            collective_id=0, has_side_effects=True, vmem_limit_bytes=60 * 1024 * 1024
+            collective_id=0, has_side_effects=True, vmem_limit_bytes=111 * 512 * 1024
         ),
-    )(meta, payload, cache, norm_gain, query_weight, query_bias, kv_weight, kv_bias)
+    )(lists, payload, cache, norm_gain, query_weight, query_bias, kv_weight, kv_bias)
 
 
 def solution(mesh):

time: 162 us -> 153 us (0.944)
  local copies, waits for them, and re-layouts: 9.78 us -> 4.64 us
  Pallas kernels: 150 us -> 145 us
    pallas_call x1, Pallas kernels: 150 us -> 145 us  [body(): pl.pallas_call(functools.partial(kernel, sections, reps, most_blk), out_s...]
    unnamed x7 -> x3, local copies, waits for them, and re-layouts: 7.19 us -> 4.64 us
where the time goes in v2:
time: 153 us; the launch traced here: 152 us
  Pallas kernels  145 us (95%)
  local copies, waits for them, and re-layouts  4.64 us (3%)
  between operations  1.93 us (1%)
    pallas_call x1, Pallas kernels, body(): pl.pallas_call(functools.partial(kernel, sections, reps, most_blk), out_s...  145 us
    unnamed x3, local copies, waits for them, and re-layouts  4.64 us

profile of v2, /device:TPU:0, one launch (start us, length us, event | category | flops | bytes accessed | tf_op | source)
XLA Modules:
  0.0 151.8 jit_solution(14739480392512565878)
XLA Ops:
  1.9 145.3 %shard_map.139 = (bf16[1,512,3584]{2,1,0:T(8,128)(2,1)S(1)}, bf16[1,512,3584]{2,1,0:T(8,128)(2,1)S(1)}, bf16[1,512,1024]{2,1,0:T(8,128)(2,1)S(1)}) custom-call(s32[1,128]{1,0:T(1,128)} %bitcast.3, s32[1,2]{1,0:T(1,128)} %bitcast.4, s32[1,2]{1,0:T(1,128)} %bitcast.5, s32[1,1]{1,0:T(1,128)S(6)} %copy.21.lists_ref_3_, s32[1,1]{1,0:T(1,128)S(6)} %copy.22.lists_ref_4_, ...), custom_call_target="tpu_custom_call" | custom-call | tf_op jit(solution)/shard_map/pallas_call | solution.py:361
  147.2 1.8 %copy.18 = bf16[1,512,3584]{2,1,0:T(8,128)(2,1)} copy(bf16[1,512,3584]{2,1,0:T(8,128)(2,1)S(1)} %get-tuple-element.3) | data formatting | bytes 7340032
  149.0 1.0 copy.20
  150.0 1.8 %copy.19 = bf16[1,512,3584]{2,1,0:T(8,128)(2,1)} copy(bf16[1,512,3584]{2,1,0:T(8,128)(2,1)S(1)} %get-tuple-element.4) | data formatting | bytes 7340032

commit v3 on v2

--- a/solution.py
+++ b/solution.py
@@ -329,6 +329,26 @@
             row_copy(j).wait_send()
 
 
+def put_out(parts, *refs):
+    count = (len(refs) - 1) // 2
+    sem = refs[-1]
+    copies = []
+    for k in range(count):
+        source, target = refs[k], refs[count + k]
+        step = source.shape[1] // parts
+        for j in range(parts):
+            here = pl.ds(j * step, step)
+            copies.append(
+                pltpu.make_async_copy(
+                    source.at[:, here, :], target.at[:, here, :], sem.at[k * parts + j]
+                )
+            )
+    for copy in copies:
+        copy.start()
+    for copy in copies:
+        copy.wait()
+
+
 def body(
     cache,
     payload,
@@ -358,7 +378,7 @@
     vmem = pl.BlockSpec(memory_space=pltpu.VMEM)
     anywhere = pl.BlockSpec(memory_space=pltpu.HBM)
     dma = pltpu.SemaphoreType.DMA
-    return pl.pallas_call(
+    results = pl.pallas_call(
         functools.partial(kernel, sections, reps, most_blk),
         out_shape=(
             pltpu.VMEM(cache.shape, cache.dtype),
@@ -389,6 +409,17 @@
             collective_id=0, has_side_effects=True, vmem_limit_bytes=111 * 512 * 1024
         ),
     )(lists, payload, cache, norm_gain, query_weight, query_bias, kv_weight, kv_bias)
+    parts = row_chunks
+    return tuple(
+        pl.pallas_call(
+            functools.partial(put_out, parts),
+            out_shape=tuple(pltpu.HBM(x.shape, x.dtype) for x in results),
+            in_specs=[vmem] * len(results),
+            out_specs=(anywhere,) * len(results),
+            scratch_shapes=[dma((parts * len(results),))],
+            compiler_params=pltpu.CompilerParams(vmem_limit_bytes=1024 * 1024),
+        )(*results)
+    )
 
 
 def solution(mesh):

time: 153 us -> 152 us (level)
  local copies, waits for them, and re-layouts: 4.64 us -> 0 us
  Pallas kernels: 145 us -> 149 us
    unnamed x3 -> x0, local copies, waits for them, and re-layouts: 4.64 us -> none
    pallas_call x0 -> x1, Pallas kernels: none -> 3.38 us  [body(): pl.pallas_call(functools.partial(put_out, parts), out_shape=tuple((pltpu....]
where the time goes in v3:
time: 152 us; the launch traced here: 151 us
  Pallas kernels  149 us (98%)
  between operations  1.93 us (1%)
    pallas_call x1, Pallas kernels, body(): pl.pallas_call(functools.partial(kernel, sections, reps, most_blk), out_s...  145 us
    pallas_call x1, Pallas kernels, body(): pl.pallas_call(functools.partial(put_out, parts), out_shape=tuple((pltpu....  3.38 us

profile of v3, /device:TPU:0, one launch (start us, length us, event | category | flops | bytes accessed | tf_op | source)
XLA Modules:
  0.0 150.6 jit_solution(5162858440625282560)
XLA Ops:
  1.9 145.3 %shard_map.139 = (bf16[1,512,3584]{2,1,0:T(8,128)(2,1)S(1)}, bf16[1,512,3584]{2,1,0:T(8,128)(2,1)S(1)}, bf16[1,512,1024]{2,1,0:T(8,128)(2,1)S(1)}) custom-call(s32[1,128]{1,0:T(1,128)} %bitcast.3, s32[1,2]{1,0:T(1,128)} %bitcast.4, s32[1,2]{1,0:T(1,128)} %bitcast.5, s32[1,1]{1,0:T(1,128)S(6)} %copy.15.lists_ref_3_, s32[1,1]{1,0:T(1,128)S(6)} %copy.16.lists_ref_4_, ...), custom_call_target="tpu_custom_call" | custom-call | tf_op jit(solution)/shard_map/pallas_call | solution.py:381
  147.2 3.4 %shard_map.140 = (bf16[1,512,3584]{2,1,0:T(8,128)(2,1)}, bf16[1,512,3584]{2,1,0:T(8,128)(2,1)}, bf16[1,512,1024]{2,1,0:T(8,128)(2,1)}) custom-call(bf16[1,512,3584]{2,1,0:T(8,128)(2,1)S(1)} %get-tuple-element.6.refs_0_, bf16[1,512,3584]{2,1,0:T(8,128)(2,1)S(1)} %get-tuple-element.7.refs_1_, bf16[1,512,1024]{2,1,0:T(8,128)(2,1)S(1)} %get-tuple-element.8.refs_2_), custom_call_target="tpu_custom_call" | custom-call | tf_op jit(solution)/shard_map/pallas_call | solution.py:414
